TPU v7x, 256 devices: a whole 4x4x8 slice. The times are simulated.
256 devices in a mesh: task: 32 (over z, y), occ: 8 (over x, core).
Axes of the slice: x: 4, y: 4, z: 8, core: 2. Of those that a mesh axis runs over, the one named last changes fastest.
Arguments:
- ao_tiles: bfloat16 [5120, 8, 32, 128], P('task'), may hold values from -6 to 6
- mo_coeffs: bfloat16 [1536, 200], P(None, 'occ'), may hold values from -0.5 to 0.5
- mu_blocks: int32 [5120], P('task'), may hold values from 0 to 191
- nu_blocks: int32 [5120], P('task'), may hold values from 0 to 47
- tile_live: int32 [5120], P('task'), may hold values 0 or 1
- batch_target: int32 [640], P('task'), may hold values from 0 to 2
- batch_count: int32 [32], P('task'), may hold values from 1 to 20
Outputs:
- half_mo: float32 [200, 200, 4096], P('occ', None, 'task')
Inputs may be any that keep to these rules, and one draw needn't show every extreme that they name: `batch_target`: the batch's kl block is the block owned by task index (own index + value) mod 32. `batch_count`: batches at or after this count in a list are not part of the work.
All inputs are finite; a program needn't handle non-finite values. No bound on the sum of `tile_live` on one device may be relied on, other than what follows from the above.
Results may differ from a plain program's by a relative error of at most 0.0029.
Values may be sent and summed in bfloat16 or wider, within the bound.
A program may use at most 128 MiB of HBM per device.

v0:
```python
from functools import partial

import jax
import jax.numpy as jnp
from jax import lax
from jax.sharding import PartitionSpec as P

SPREAD = 3


def sent_to_all(array, axis):
    length = lax.axis_size(axis)
    return lax.all_to_all(
        jnp.broadcast_to(array[None], (length, *array.shape)), axis, 0, 0, tiled=True
    )


def in_order(blocks, dim):
    dims = list(blocks.shape[1:])
    dims[dim] *= blocks.shape[0]
    return jnp.moveaxis(blocks, 0, dim).reshape(dims)


def gather_directly(array, axis, dim):
    blocks = sent_to_all(array, axis)
    return in_order(blocks, dim)


def from_behind(block, axis, distance):
    devices = range(lax.axis_size(axis))
    route = [((i - distance) % len(devices), i) for i in devices]
    return lax.ppermute(block, axis, route)


def local(ao_tiles, mo_coeffs, mu_blocks, nu_blocks, tile_live, batch_target, batch_count):
    coeff_all = gather_directly(mo_coeffs, "occ", 1)
    mu_width = ao_tiles.shape[1]
    nu_width = ao_tiles.shape[2]
    kl_width = ao_tiles.shape[3]
    batches = batch_target.shape[0]
    per_batch = ao_tiles.shape[0] // batches
    local_occ = mo_coeffs.shape[1]
    all_occ = coeff_all.shape[1]
    tiles_all = ao_tiles.reshape(batches, per_batch, mu_width, nu_width, kl_width)
    mu_rows = mu_blocks.reshape(batches, per_batch)[:, :, None] * mu_width + jnp.arange(
        mu_width, dtype=jnp.int32
    )
    nu_rows = nu_blocks.reshape(batches, per_batch)[:, :, None] * nu_width + jnp.arange(
        nu_width, dtype=jnp.int32
    )
    weights = tile_live.reshape(batches, per_batch).astype(jnp.bfloat16)
    listed = batch_count[0]

    def contract(batch_index):
        tile_block = lax.dynamic_index_in_dim(tiles_all, batch_index, 0, keepdims=False)
        coeff_mu = mo_coeffs[lax.dynamic_index_in_dim(mu_rows, batch_index, 0, keepdims=False)]
        quarter = jnp.einsum(
            "bmi,bmnk->bink", coeff_mu, tile_block, preferred_element_type=jnp.float32
        ).astype(jnp.bfloat16)
        kept_tiles = lax.dynamic_index_in_dim(weights, batch_index, 0, keepdims=False)
        coeff_nu = (
            coeff_all[lax.dynamic_index_in_dim(nu_rows, batch_index, 0, keepdims=False)]
            * kept_tiles[:, None, None]
        )
        return jnp.einsum("bnj,bink->ijk", coeff_nu, quarter, preferred_element_type=jnp.float32)

    def visit_batch(selection, batch_index, partials):
        target = batch_target[batch_index]

        def add_batch(current):
            earlier = lax.dynamic_index_in_dim(current, target, 0, keepdims=False)
            return lax.dynamic_update_index_in_dim(
                current, earlier + contract(batch_index), target, 0
            )

        wanted = target > 0 if selection == 1 else target == 0
        return lax.cond(wanted, add_batch, lambda current: current, partials)

    empty = jnp.zeros((SPREAD, local_occ, all_occ, kl_width), jnp.float32)
    partials = lax.fori_loop(0, listed, partial(visit_batch, 1), empty)
    arrived = jnp.zeros((local_occ, all_occ, kl_width), jnp.float32)
    for spread_index in range(1, SPREAD):
        arrived = arrived + from_behind(partials[spread_index], "task", spread_index)
    partials = lax.fori_loop(0, listed, partial(visit_batch, 2), partials)
    return partials[0] + arrived


def solution(mesh):
    in_specs = (
        P("task", None, None, None),
        P(None, "occ"),
        P("task"),
        P("task"),
        P("task"),
        P("task"),
        P("task"),
    )
    out_specs = P("occ", None, "task")
    return jax.shard_map(local, mesh=mesh, in_specs=in_specs, out_specs=out_specs, check_vma=False)
```

profile of v0, /device:TPU:64, one launch (start us, length us, event | category | flops | bytes accessed | tf_op | source)
XLA Modules:
  0.0 366.3 jit_solution(12242608561110302819)
XLA Ops:
  7.6 11.7 %all-to-all-done = bf16[8,1536,25]{1,2,0:T(8,128)(2,1)S(1)} async-done(((bf16[8,1536,25]{1,2,0:T(8,128)(2,1)}), bf16[8,1536,25]{1,2,0:T(8,128)(2,1)S(1)}, u32[]{:S(2)}, u32[]{:S(2)}) %all-to-all-start) | async-done | bytes 614432 | tf_op jit(solution)/shard_map/all_to_all | solution.py:13
  23.3 218.5 %while.28 = (s32[]{:T(128)}, f32[3,25,200,128]{3,2,1,0:T(8,128)}, s32[]{:T(128)}, s32[20]{0:T(128)S(1)}, bf16[1536,25]{1,0:T(8,128)(2,1)S(1)}, /*index=5*/bf16[2...) while((s32[]{:T(128)}, f32[3,25,200,128]{3,2,1,0:T(8,128)}, ...), condition=%wide.region_3.4_spmd.clone, body=%wide.region_0.3_spmd.clone.sunk | while | flops 341481728 | bytes 15448561 | solution.py:80
  25.4 10.4 %conditional.6 = (f32[3,25,200,128]{3,2,1,0:T(8,128)}) conditional(s32[]{:T(128)} %convert_element_type.28, f32[3,25,200,128]{3,2,1,0:T(8,128)} %get-tuple-element.463, (s32[]{:T(128)}, f32[3,25,200,128]{3,2,1,0:T(8,128)}, s32[]{:T(128)}, s32[20,8]{1,0:T(8,128)S(1)}, bf16[1536,25]{1,0:T(8,128)(2,1)S(1)}, ...), branch_computations={%region_1.0_spmd, %region_2.2_spmd} | conditional | flops 341481728 | bytes 15422680 | solution.py:77
  37.8 10.4 %conditional.6 = (f32[3,25,200,128]{3,2,1,0:T(8,128)}) conditional(s32[]{:T(128)} %convert_element_type.28, f32[3,25,200,128]{3,2,1,0:T(8,128)} %get-tuple-element.463, (s32[]{:T(128)}, f32[3,25,200,128]{3,2,1,0:T(8,128)}, s32[]{:T(128)}, s32[20,8]{1,0:T(8,128)S(1)}, bf16[1536,25]{1,0:T(8,128)(2,1)S(1)}, ...), branch_computations={%region_1.0_spmd, %region_2.2_spmd} | conditional | flops 341481728 | bytes 15422680 | solution.py:77
  50.3 10.4 %conditional.6 = (f32[3,25,200,128]{3,2,1,0:T(8,128)}) conditional(s32[]{:T(128)} %convert_element_type.28, f32[3,25,200,128]{3,2,1,0:T(8,128)} %get-tuple-element.463, (s32[]{:T(128)}, f32[3,25,200,128]{3,2,1,0:T(8,128)}, s32[]{:T(128)}, s32[20,8]{1,0:T(8,128)S(1)}, bf16[1536,25]{1,0:T(8,128)(2,1)S(1)}, ...), branch_computations={%region_1.0_spmd, %region_2.2_spmd} | conditional | flops 341481728 | bytes 15422680 | solution.py:77
  62.7 10.4 %conditional.6 = (f32[3,25,200,128]{3,2,1,0:T(8,128)}) conditional(s32[]{:T(128)} %convert_element_type.28, f32[3,25,200,128]{3,2,1,0:T(8,128)} %get-tuple-element.463, (s32[]{:T(128)}, f32[3,25,200,128]{3,2,1,0:T(8,128)}, s32[]{:T(128)}, s32[20,8]{1,0:T(8,128)S(1)}, bf16[1536,25]{1,0:T(8,128)(2,1)S(1)}, ...), branch_computations={%region_1.0_spmd, %region_2.2_spmd} | conditional | flops 341481728 | bytes 15422680 | solution.py:77
  75.2 10.4 %conditional.6 = (f32[3,25,200,128]{3,2,1,0:T(8,128)}) conditional(s32[]{:T(128)} %convert_element_type.28, f32[3,25,200,128]{3,2,1,0:T(8,128)} %get-tuple-element.463, (s32[]{:T(128)}, f32[3,25,200,128]{3,2,1,0:T(8,128)}, s32[]{:T(128)}, s32[20,8]{1,0:T(8,128)S(1)}, bf16[1536,25]{1,0:T(8,128)(2,1)S(1)}, ...), branch_computations={%region_1.0_spmd, %region_2.2_spmd} | conditional | flops 341481728 | bytes 15422680 | solution.py:77
  87.6 10.4 %conditional.6 = (f32[3,25,200,128]{3,2,1,0:T(8,128)}) conditional(s32[]{:T(128)} %convert_element_type.28, f32[3,25,200,128]{3,2,1,0:T(8,128)} %get-tuple-element.463, (s32[]{:T(128)}, f32[3,25,200,128]{3,2,1,0:T(8,128)}, s32[]{:T(128)}, s32[20,8]{1,0:T(8,128)S(1)}, bf16[1536,25]{1,0:T(8,128)(2,1)S(1)}, ...), branch_computations={%region_1.0_spmd, %region_2.2_spmd} | conditional | flops 341481728 | bytes 15422680 | solution.py:77
  100.1 10.4 %conditional.6 = (f32[3,25,200,128]{3,2,1,0:T(8,128)}) conditional(s32[]{:T(128)} %convert_element_type.28, f32[3,25,200,128]{3,2,1,0:T(8,128)} %get-tuple-element.463, (s32[]{:T(128)}, f32[3,25,200,128]{3,2,1,0:T(8,128)}, s32[]{:T(128)}, s32[20,8]{1,0:T(8,128)S(1)}, bf16[1536,25]{1,0:T(8,128)(2,1)S(1)}, ...), branch_computations={%region_1.0_spmd, %region_2.2_spmd} | conditional | flops 341481728 | bytes 15422680 | solution.py:77
  112.5 10.4 %conditional.6 = (f32[3,25,200,128]{3,2,1,0:T(8,128)}) conditional(s32[]{:T(128)} %convert_element_type.28, f32[3,25,200,128]{3,2,1,0:T(8,128)} %get-tuple-element.463, (s32[]{:T(128)}, f32[3,25,200,128]{3,2,1,0:T(8,128)}, s32[]{:T(128)}, s32[20,8]{1,0:T(8,128)S(1)}, bf16[1536,25]{1,0:T(8,128)(2,1)S(1)}, ...), branch_computations={%region_1.0_spmd, %region_2.2_spmd} | conditional | flops 341481728 | bytes 15422680 | solution.py:77
  125.0 10.4 %conditional.6 = (f32[3,25,200,128]{3,2,1,0:T(8,128)}) conditional(s32[]{:T(128)} %convert_element_type.28, f32[3,25,200,128]{3,2,1,0:T(8,128)} %get-tuple-element.463, (s32[]{:T(128)}, f32[3,25,200,128]{3,2,1,0:T(8,128)}, s32[]{:T(128)}, s32[20,8]{1,0:T(8,128)S(1)}, bf16[1536,25]{1,0:T(8,128)(2,1)S(1)}, ...), branch_computations={%region_1.0_spmd, %region_2.2_spmd} | conditional | flops 341481728 | bytes 15422680 | solution.py:77
  137.4 10.4 %conditional.6 = (f32[3,25,200,128]{3,2,1,0:T(8,128)}) conditional(s32[]{:T(128)} %convert_element_type.28, f32[3,25,200,128]{3,2,1,0:T(8,128)} %get-tuple-element.463, (s32[]{:T(128)}, f32[3,25,200,128]{3,2,1,0:T(8,128)}, s32[]{:T(128)}, s32[20,8]{1,0:T(8,128)S(1)}, bf16[1536,25]{1,0:T(8,128)(2,1)S(1)}, ...), branch_computations={%region_1.0_spmd, %region_2.2_spmd} | conditional | flops 341481728 | bytes 15422680 | solution.py:77
  151.9 10.4 %conditional.6 = (f32[3,25,200,128]{3,2,1,0:T(8,128)}) conditional(s32[]{:T(128)} %convert_element_type.28, f32[3,25,200,128]{3,2,1,0:T(8,128)} %get-tuple-element.463, (s32[]{:T(128)}, f32[3,25,200,128]{3,2,1,0:T(8,128)}, s32[]{:T(128)}, s32[20,8]{1,0:T(8,128)S(1)}, bf16[1536,25]{1,0:T(8,128)(2,1)S(1)}, ...), branch_computations={%region_1.0_spmd, %region_2.2_spmd} | conditional | flops 341481728 | bytes 15422680 | solution.py:77
  164.4 10.4 %conditional.6 = (f32[3,25,200,128]{3,2,1,0:T(8,128)}) conditional(s32[]{:T(128)} %convert_element_type.28, f32[3,25,200,128]{3,2,1,0:T(8,128)} %get-tuple-element.463, (s32[]{:T(128)}, f32[3,25,200,128]{3,2,1,0:T(8,128)}, s32[]{:T(128)}, s32[20,8]{1,0:T(8,128)S(1)}, bf16[1536,25]{1,0:T(8,128)(2,1)S(1)}, ...), branch_computations={%region_1.0_spmd, %region_2.2_spmd} | conditional | flops 341481728 | bytes 15422680 | solution.py:77
  176.8 10.4 %conditional.6 = (f32[3,25,200,128]{3,2,1,0:T(8,128)}) conditional(s32[]{:T(128)} %convert_element_type.28, f32[3,25,200,128]{3,2,1,0:T(8,128)} %get-tuple-element.463, (s32[]{:T(128)}, f32[3,25,200,128]{3,2,1,0:T(8,128)}, s32[]{:T(128)}, s32[20,8]{1,0:T(8,128)S(1)}, bf16[1536,25]{1,0:T(8,128)(2,1)S(1)}, ...), branch_computations={%region_1.0_spmd, %region_2.2_spmd} | conditional | flops 341481728 | bytes 15422680 | solution.py:77
  189.3 10.4 %conditional.6 = (f32[3,25,200,128]{3,2,1,0:T(8,128)}) conditional(s32[]{:T(128)} %convert_element_type.28, f32[3,25,200,128]{3,2,1,0:T(8,128)} %get-tuple-element.463, (s32[]{:T(128)}, f32[3,25,200,128]{3,2,1,0:T(8,128)}, s32[]{:T(128)}, s32[20,8]{1,0:T(8,128)S(1)}, bf16[1536,25]{1,0:T(8,128)(2,1)S(1)}, ...), branch_computations={%region_1.0_spmd, %region_2.2_spmd} | conditional | flops 341481728 | bytes 15422680 | solution.py:77
  203.8 10.4 %conditional.6 = (f32[3,25,200,128]{3,2,1,0:T(8,128)}) conditional(s32[]{:T(128)} %convert_element_type.28, f32[3,25,200,128]{3,2,1,0:T(8,128)} %get-tuple-element.463, (s32[]{:T(128)}, f32[3,25,200,128]{3,2,1,0:T(8,128)}, s32[]{:T(128)}, s32[20,8]{1,0:T(8,128)S(1)}, bf16[1536,25]{1,0:T(8,128)(2,1)S(1)}, ...), branch_computations={%region_1.0_spmd, %region_2.2_spmd} | conditional | flops 341481728 | bytes 15422680 | solution.py:77
  216.2 10.4 %conditional.6 = (f32[3,25,200,128]{3,2,1,0:T(8,128)}) conditional(s32[]{:T(128)} %convert_element_type.28, f32[3,25,200,128]{3,2,1,0:T(8,128)} %get-tuple-element.463, (s32[]{:T(128)}, f32[3,25,200,128]{3,2,1,0:T(8,128)}, s32[]{:T(128)}, s32[20,8]{1,0:T(8,128)S(1)}, bf16[1536,25]{1,0:T(8,128)(2,1)S(1)}, ...), branch_computations={%region_1.0_spmd, %region_2.2_spmd} | conditional | flops 341481728 | bytes 15422680 | solution.py:77
  230.8 10.4 %conditional.6 = (f32[3,25,200,128]{3,2,1,0:T(8,128)}) conditional(s32[]{:T(128)} %convert_element_type.28, f32[3,25,200,128]{3,2,1,0:T(8,128)} %get-tuple-element.463, (s32[]{:T(128)}, f32[3,25,200,128]{3,2,1,0:T(8,128)}, s32[]{:T(128)}, s32[20,8]{1,0:T(8,128)S(1)}, bf16[1536,25]{1,0:T(8,128)(2,1)S(1)}, ...), branch_computations={%region_1.0_spmd, %region_2.2_spmd} | conditional | flops 341481728 | bytes 15422680 | solution.py:77
  247.0 72.4 %while.29 = (s32[]{:T(128)}, f32[3,25,200,128]{3,2,1,0:T(8,128)}, s32[]{:T(128)}, s32[20]{0:T(128)S(1)}, bf16[1536,25]{1,0:T(8,128)(2,1)S(1)}, /*index=5*/bf16[2...) while((s32[]{:T(128)}, f32[3,25,200,128]{3,2,1,0:T(8,128)}, ...), condition=%wide.region_7.8_spmd.clone, body=%wide.region_4.7_spmd.clone.sunk | while | flops 341481728 | bytes 15448561 | solution.py:84
  269.4 10.3 %conditional.7 = (f32[3,25,200,128]{3,2,1,0:T(8,128)}) conditional(s32[]{:T(128)} %convert_element_type.29, f32[3,25,200,128]{3,2,1,0:T(8,128)} %get-tuple-element.502, (s32[]{:T(128)}, f32[3,25,200,128]{3,2,1,0:T(8,128)}, s32[]{:T(128)}, s32[20,8]{1,0:T(8,128)S(1)}, bf16[1536,25]{1,0:T(8,128)(2,1)S(1)}, ...), branch_computations={%region_5.5_spmd, %region_6.6_spmd} | conditional | flops 341481728 | bytes 15422680 | solution.py:77
  290.0 10.3 %conditional.7 = (f32[3,25,200,128]{3,2,1,0:T(8,128)}) conditional(s32[]{:T(128)} %convert_element_type.29, f32[3,25,200,128]{3,2,1,0:T(8,128)} %get-tuple-element.502, (s32[]{:T(128)}, f32[3,25,200,128]{3,2,1,0:T(8,128)}, s32[]{:T(128)}, s32[20,8]{1,0:T(8,128)S(1)}, bf16[1536,25]{1,0:T(8,128)(2,1)S(1)}, ...), branch_computations={%region_5.5_spmd, %region_6.6_spmd} | conditional | flops 341481728 | bytes 15422680 | solution.py:77
  306.4 10.3 %conditional.7 = (f32[3,25,200,128]{3,2,1,0:T(8,128)}) conditional(s32[]{:T(128)} %convert_element_type.29, f32[3,25,200,128]{3,2,1,0:T(8,128)} %get-tuple-element.502, (s32[]{:T(128)}, f32[3,25,200,128]{3,2,1,0:T(8,128)}, s32[]{:T(128)}, s32[20,8]{1,0:T(8,128)S(1)}, bf16[1536,25]{1,0:T(8,128)(2,1)S(1)}, ...), branch_computations={%region_5.5_spmd, %region_6.6_spmd} | conditional | flops 341481728 | bytes 15422680 | solution.py:77
  319.4 31.6 %collective-permute-done.1 = f32[25,200,128]{2,1,0:T(8,128)} collective-permute-done((f32[25,200,128]{2,1,0:T(8,128)}, f32[25,200,128]{2,1,0:T(8,128)}, u32[]{:S(2)}, u32[]{:S(2)}) %collective-permute-start.1) | collective-permute-done | bytes 2560032 | tf_op jit(solution)/shard_map/ppermute | solution.py:32
  (445 shorter events, 224.3 us)
Async XLA Ops:
  0.0 7.3 %copy-start.2 = (s32[160]{0:T(256)S(1)}, s32[160]{0:T(256)}, u32[]{:S(2)}) copy-start(s32[160]{0:T(256)} %param.19) | copy-start | bytes 1924
  0.0 7.4 %copy-start = (s32[160]{0:T(256)S(1)}, s32[160]{0:T(256)}, u32[]{:S(2)}) copy-start(s32[160]{0:T(256)} %param.18) | copy-start | bytes 1924
  0.0 7.5 %copy-start.1 = (s32[160]{0:T(256)S(1)}, s32[160]{0:T(256)}, u32[]{:S(2)}) copy-start(s32[160]{0:T(256)} %param.17) | copy-start | bytes 1924
  1.9 17.4 %all-to-all-start = ((bf16[8,1536,25]{1,2,0:T(8,128)(2,1)}), bf16[8,1536,25]{1,2,0:T(8,128)(2,1)S(1)}, u32[]{:S(2)}, u32[]{:S(2)}) async-start(bf16[8,1536,25]{1,2,0:T(8,128)(2,1)} %broadcast_in_dim.15), calls=%async_computation | async-start | bytes 1572864 | tf_op jit(solution)/shard_map/all_to_all | solution.py:13
  19.8 3.5 copy-start.3
  247.0 104.1 %collective-permute-start.1 = (f32[25,200,128]{2,1,0:T(8,128)}, f32[25,200,128]{2,1,0:T(8,128)}, u32[]{:S(2)}, u32[]{:S(2)}) collective-permute-start(f32[25,200,128]{2,1,0:T(8,128)} %get-tuple-element.323), channel_id=1, source_target_pairs={{240,0},{248,8},{0,16},{8,24},{16,32},{24,40},{32,48},{40,56},{48,... | collective-permute-start | bytes 7680008 | tf_op jit(solution)/shard_map/ppermute | solution.py:32
  247.0 114.3 %collective-permute-start = (f32[25,200,128]{2,1,0:T(8,128)}, f32[25,200,128]{2,1,0:T(8,128)}, u32[]{:S(2)}, u32[]{:S(2)}) collective-permute-start(f32[25,200,128]{2,1,0:T(8,128)} %get-tuple-element.324), channel_id=1, source_target_pairs={{248,0},{0,8},{8,16},{16,24},{24,32},{32,40},{40,48},{48,56},{56,6... | collective-permute-start | bytes 7680008 | tf_op jit(solution)/shard_map/ppermute | solution.py:32
where the time goes:
time: 360 us; the launch traced here: 366 us
  local copies, waits for them, and re-layouts  138 us (38%)
  loops' own time  98.9 us (27%)
  matrix products  62.8 us (17%)
  waiting for transfers between devices  53.5 us (15%)
  other arithmetic  8.29 us (2%)
  starting transfers between devices  4.31 us (1%)
    dot_general x20, matrix products, contract(): jnp.einsum('bnj,bink->ijk', coeff_nu, quarter, preferred_element_type=jnp...  47.7 us
    another operation x40, loops' own time, visit_batch(): return lax.cond(wanted, add_batch, lambda current: current, partials)  42.8 us
    ppermute x2, waiting for transfers between devices, from_behind(): return lax.ppermute(block, axis, route)  41.8 us
    dynamic_slice x20, local copies, waits for them, and re-layouts, add_batch(): earlier = lax.dynamic_index_in_dim(current, target, 0, keepdims=False)  37.9 us
    another operation x1, loops' own time, local(): partials = lax.fori_loop(0, listed, partial(visit_batch, 1), empty)  28.3 us
    another operation x1, loops' own time, local(): partials = lax.fori_loop(0, listed, partial(visit_batch, 2), partials)  27.9 us
    dynamic_slice x40, local copies, waits for them, and re-layouts, visit_batch(): target = batch_target[batch_index]  26.3 us
    gather x20, local copies, waits for them, and re-layouts, contract(): coeff_all[lax.dynamic_index_in_dim(nu_rows, batch_index, 0, keepdims=False)]  23.1 us
  transfers between devices with their start and end apart: 3, of which 3 were waited for; matrix products, arithmetic and copies ran while one was open for 11% of the time, Pallas kernels for 0%

commit v1 on v0

v1 whole, which is shorter than its diff:
```python
import jax
import jax.numpy as jnp
from jax import lax
from jax.experimental import pallas as pl
from jax.experimental.pallas import tpu as pltpu
from jax.sharding import PartitionSpec as P

MESH = pl.DeviceIdType.MESH
SPREAD, MUT, NUT, KLW = 3, 8, 32, 128
NB, BATCH = 20, 8
TILES = NB * BATCH
NOCC, LOCAL, BLOCKS_MU = 200, 25, 192
DEPTH = TILES * NUT
STEP = 16
PIECES = 5

VMEM_LIMIT = 60 << 20
WIDTH = 4
FULL = LOCAL // WIDTH
COUNT = FULL + 1
SPLIT = 128


def kernel(
    mu_ref, nu_ref, live_ref, target_ref, count_ref, own_ref, tiles_hbm, out_ref,
    tiles, spread, gathered, staged, turned, across, quarter, held, send_two, send_one, mid, from_one, from_two,
    load_sem, own_sem, gather_send, gather_recv, send_sem, recv_sem,
):
    task, occ = lax.axis_index("task"), lax.axis_index("occ")
    z, y = task // 4, task % 4
    up, down = (y + 1) % 4, (y + 3) % 4
    after = (task + 1) % 32
    before = (task + 31) % 32
    minus, minus_from = z * 4 + down, z * 4 + up
    jump = ((y + 1) // 2) % 2
    last_hop = ((z + jump) % 8) * 4 + down
    jumped = ((up + 1) // 2) % 2
    last_from = ((z + 8 - jumped) % 8) * 4 + up
    x, core = occ // 2, occ % 2
    partner = x * 2 + 1 - core

    per_piece = TILES // PIECES

    def load(piece):
        return pltpu.make_async_copy(
            tiles_hbm.at[pl.ds(piece * per_piece, per_piece)],
            tiles.at[pl.ds(piece * per_piece, per_piece)],
            load_sem.at[piece],
        )

    for piece in range(PIECES):
        load(piece).start()

    barrier = pltpu.get_barrier_semaphore()
    for other in (after, before, minus, minus_from, last_hop, last_from):
        pl.semaphore_signal(barrier, inc=1, device_id={"task": other}, device_id_type=MESH)
    for other in (partner, (x + 1) % 4 * 2 + core, (x + 2) % 4 * 2 + core, (x + 3) % 4 * 2 + core):
        pl.semaphore_signal(barrier, inc=1, device_id={"occ": other}, device_id_type=MESH)
    pl.semaphore_wait(barrier, 10)

    def give(source, slot, index, other):
        return pltpu.make_async_remote_copy(
            src_ref=source, dst_ref=gathered.at[core, slot],
            send_sem=gather_send.at[index], recv_sem=gather_recv.at[index],
            device_id={"occ": other}, device_id_type=MESH,
        )

    def direct(d):
        return give(own_ref, x, d, (x + d) % 4 * 2 + core)

    def across_chip(d):
        slot = (x + 4 - d) % 4
        return give(own_ref if d == 0 else gathered.at[core, slot], slot, 4 + d, partner)

    for d in (2, 1, 3):
        direct(d).start()
    across_chip(0).start()
    keep_own = pltpu.make_async_copy(own_ref, gathered.at[core, x], own_sem)
    keep_own.start()

    row = lax.broadcasted_iota(jnp.int32, (128, 128), 0)
    lane = lax.broadcasted_iota(jnp.int32, (128, 128), 1)
    spreader = jnp.concatenate(
        [
            jnp.where(row == lane // 16 + 8 * v, 1.0, 0.0).astype(jnp.bfloat16)
            for v in range(16)
        ],
        axis=1,
    )

    def spread_block(block, carry):
        part = own_ref[:, pl.ds(pl.multiple_of(block * 128, 128), 128)]
        wide = jnp.dot(part, spreader, preferred_element_type=jnp.float32)
        for v in range(16):
            spread[block * 16 + v, :LOCAL] = wide[:, 128 * v : 128 * v + 128]
        return carry

    lax.fori_loop(0, 12, spread_block, 0)

    row = lax.broadcasted_iota(jnp.int32, (16, 128), 0)
    lane = lax.broadcasted_iota(jnp.int32, (16, 128), 1)
    diagonal = jnp.where(lane % 16 == row, 1.0, 0.0).astype(jnp.bfloat16)

    def quarters(first, width, step):
        for u in range(STEP):
            g = step * STEP + u
            mu = mu_ref[g]
            left = jnp.concatenate(
                [
                    jnp.broadcast_to(spread[mu, pl.ds(first + i, 1), :], (16, 128)).astype(
                        jnp.bfloat16
                    )
                    * diagonal
                    for i in range(width)
                ],
                axis=0,
            )
            block = tiles[g]
            right = jnp.concatenate(
                [block[:, 16 * q : 16 * q + 16].reshape(128, 128) for q in range(2)], axis=1
            )
            product = jnp.dot(left, right, preferred_element_type=jnp.float32)
            product = product.astype(jnp.bfloat16).reshape(width, 16, 256)
            for q in range(2):
                quarter[:width, pl.ds(pl.multiple_of(g * 32 + 16 * q, 16), 16), :] = product[
                    :, :, 128 * q : 128 * q + 128
                ]

    def all_quarters(first, width):
        def inner(step, carry):
            quarters(first, width, step)
            return carry

        lax.fori_loop(0, TILES // STEP, inner, 0)

    for d in (1, 3, 2):
        direct(d).wait_recv()
        across_chip(d).start()
    for piece in range(PIECES):
        load(piece).wait()
    all_quarters(0, WIDTH)
    keep_own.wait()
    for d in range(4):
        across_chip(d).wait_recv()

    def turn(block, carry):
        where = pl.ds(pl.multiple_of(block * 128, 128), 128)
        for o in range(8):
            staged[25 * o : 25 * o + 25, :] = gathered[o % 2, o // 2, :, where].astype(jnp.float32)
        wide = staged[...]
        turned[0, block] = wide.astype(jnp.bfloat16)
        for r in range(1, 4):
            turned[r, block] = pltpu.roll(wide, 32 * r, 1).astype(jnp.bfloat16)
        return carry

    lax.fori_loop(0, 12, turn, 0)

    lanes = lax.broadcasted_iota(jnp.int32, (NOCC, 128), 1) // 32
    line = lax.broadcasted_iota(jnp.int32, (8, 128), 1) // 32
    listed = count_ref[0]

    def gather(group, carry):
        batch = group // 2
        merged = None
        kept = jnp.zeros((8, 128), jnp.int32)
        for u in range(4):
            g = group * 4 + u
            nu = nu_ref[g]
            part = turned[(u + 4 - nu % 4) % 4, nu // 4].astype(jnp.float32)
            merged = part if u == 0 else jnp.where(lanes == u, part, merged)
            kept = jnp.where(line == u, live_ref[g], kept)
        where = pl.ds(pl.multiple_of(group * 128, 128), 128)
        target = target_ref[batch]
        for s in range(SPREAD):
            chosen = jnp.where(target == s, jnp.where(batch < listed, 1, 0), 0)
            scale = (kept * chosen).astype(jnp.float32)[:1]
            across[s, :, where] = (merged * scale).astype(jnp.bfloat16)
        return carry

    lax.fori_loop(0, TILES // 4, gather, 0)

    def partial_sum(s, width):
        right = jnp.concatenate([quarter[i] for i in range(width)], axis=1)
        return jnp.dot(across[s], right, preferred_element_type=jnp.float32)

    def copy(source, target, kind, chunk, width, low, high, device):
        box = (pl.ds(chunk * WIDTH, width), pl.ds(low, high - low))
        return pltpu.make_async_remote_copy(
            src_ref=source.at[box], dst_ref=target.at[box],
            send_sem=send_sem.at[kind, chunk], recv_sem=recv_sem.at[kind, chunk],
            device_id={"task": device}, device_id_type=MESH,
        )

    def copy_one(chunk, width):
        return copy(send_one, from_one, 0, chunk, width, 0, SPLIT, after)

    def copy_two(chunk, width):
        return copy(send_two, mid, 1, chunk, width, 0, SPLIT, minus)

    def copy_on(chunk, width):
        return copy(mid, from_two, 2, chunk, width, 0, SPLIT, last_hop)

    def copy_through(chunk, width):
        return copy(send_two, mid, 3, chunk, width, SPLIT, NOCC, after)

    def copy_sum(chunk, width):
        return copy(send_one, from_one, 4, chunk, width, SPLIT, NOCC, after)

    def relay(chunk, width):
        copy_two(chunk, width).wait_recv()
        copy_on(chunk, width).start()
        copy_through(chunk, width).wait_recv()
        for i in range(width):
            at = chunk * WIDTH + i
            send_one[at, SPLIT:] = (held[at] + mid[at, SPLIT:].astype(jnp.float32)).astype(jnp.bfloat16)
        copy_sum(chunk, width).start()

    def finish(chunk, width):
        copy_one(chunk, width).wait_recv()
        copy_on(chunk, width).wait_recv()
        copy_sum(chunk, width).wait_recv()
        for i in range(width):
            at = chunk * WIDTH + i
            out_ref[at] = out_ref[at] + from_one[at].astype(jnp.float32)
            out_ref[at, :SPLIT] = out_ref[at, :SPLIT] + from_two[at, :SPLIT].astype(jnp.float32)

    def sums(chunk, width, between):
        total = partial_sum(2, width)
        for i in range(width):
            send_two[chunk * WIDTH + i] = total[:, 128 * i : 128 * i + 128].astype(jnp.bfloat16)
        copy_two(chunk, width).start()
        copy_through(chunk, width).start()
        between()
        total = partial_sum(1, width)
        for i in range(width):
            part = total[:, 128 * i : 128 * i + 128]
            send_one[chunk * WIDTH + i, :SPLIT] = part[:SPLIT].astype(jnp.bfloat16)
            held[chunk * WIDTH + i] = part[SPLIT:]
        copy_one(chunk, width).start()
        total = partial_sum(0, width)
        for i in range(width):
            out_ref[chunk * WIDTH + i] = total[:, 128 * i : 128 * i + 128]

    def body(chunk, carry):
        def between():
            @pl.when(chunk > 0)
            def _():
                relay(chunk - 1, WIDTH)

        sums(chunk, WIDTH, between)

        @pl.when(chunk < FULL - 1)
        def _():
            all_quarters(chunk * WIDTH + WIDTH, WIDTH)

        return carry

    lax.fori_loop(0, FULL, body, 0)
    all_quarters(FULL * WIDTH, 1)
    sums(FULL, 1, lambda: relay(FULL - 1, WIDTH))
    relay(FULL, 1)

    def ending(chunk, carry):
        finish(chunk, WIDTH)
        return carry

    lax.fori_loop(0, FULL, ending, 0)
    finish(FULL, 1)

    def sent(chunk, width):
        for copies in (copy_one, copy_two, copy_on, copy_through, copy_sum):
            copies(chunk, width).wait_send()

    def drain(chunk, carry):
        sent(chunk, WIDTH)
        return carry

    lax.fori_loop(0, FULL, drain, 0)
    sent(FULL, 1)
    for d in (1, 2, 3):
        direct(d).wait_send()
    for d in range(4):
        across_chip(d).wait_send()


def local(ao_tiles, mo_coeffs, mu_blocks, nu_blocks, tile_live, batch_target, batch_count):
    smem = pl.BlockSpec(memory_space=pltpu.SMEM)
    vmem = pl.BlockSpec(memory_space=pltpu.VMEM)
    lists = pltpu.VMEM((LOCAL, NOCC, KLW), jnp.bfloat16)
    return pl.pallas_call(
        kernel,
        out_shape=jax.ShapeDtypeStruct((LOCAL, NOCC, KLW), jnp.float32),
        in_specs=[smem] * 5 + [vmem, pl.BlockSpec(memory_space=pl.ANY)],
        out_specs=vmem,
        scratch_shapes=[
            pltpu.VMEM((TILES, MUT, NUT, KLW), jnp.bfloat16),
            pltpu.VMEM((BLOCKS_MU, 32, 128), jnp.float32),
            pltpu.VMEM((2, 4, LOCAL, BLOCKS_MU * MUT), jnp.bfloat16),
            pltpu.VMEM((NOCC, 128), jnp.float32),
            pltpu.VMEM((4, 12, NOCC, 128), jnp.bfloat16),
            pltpu.VMEM((SPREAD, NOCC, DEPTH), jnp.bfloat16),
            pltpu.VMEM((WIDTH, DEPTH, KLW), jnp.bfloat16),
            pltpu.VMEM((LOCAL, NOCC - SPLIT, KLW), jnp.float32),
            lists, lists, lists, lists, lists,
            pltpu.SemaphoreType.DMA((PIECES,)),
            pltpu.SemaphoreType.DMA,
            pltpu.SemaphoreType.DMA((8,)),
            pltpu.SemaphoreType.DMA((8,)),
            pltpu.SemaphoreType.DMA((5, COUNT)),
            pltpu.SemaphoreType.DMA((5, COUNT)),
        ],
        compiler_params=pltpu.CompilerParams(
            vmem_limit_bytes=VMEM_LIMIT, collective_id=0, has_side_effects=True
        ),
    )(mu_blocks, nu_blocks, tile_live, batch_target, batch_count, mo_coeffs.T, ao_tiles)


def solution(mesh):
    in_specs = (
        P("task", None, None, None),
        P(None, "occ"),
        P("task"),
        P("task"),
        P("task"),
        P("task"),
        P("task"),
    )
    out_specs = P("occ", None, "task")
    return jax.shard_map(local, mesh=mesh, in_specs=in_specs, out_specs=out_specs, check_vma=False)
```

time: 360 us -> 80.7 us (0.22)
  the two profiles are of different devices: /device:TPU:64 before, /device:TPU:1 now
where the time goes in v1:
time: 80.7 us; the launch traced here: 79.3 us
  Pallas kernels  75.3 us (93%)
  local copies, waits for them, and re-layouts  3.36 us (4%)
    pallas_call x1, Pallas kernels, local(): pl.pallas_call(kernel, out_shape=jax.ShapeDtypeStruct((LOCAL, NOCC, KLW),...  75.3 us
    unnamed x1, local copies, waits for them, and re-layouts  3.36 us

profile of v1, /device:TPU:1, one launch (start us, length us, event | category | flops | bytes accessed | tf_op | source)
XLA Modules:
  0.0 79.3 jit_solution(10391018558277861665)
XLA Ops:
  0.7 75.3 %shard_map.73 = f32[25,200,128]{2,1,0:T(8,128)} custom-call(s32[160]{0:T(256)} %mu_ref.1, s32[160]{0:T(256)} %nu_ref.1, s32[160]{0:T(256)} %live_ref.1, s32[20]{0:T(128)} %target_ref.1, s32[1]{0:T(128)S(6)} %copy.9.count_ref, bf16[25,1536]{1,0:T(8,128)(2,1)} %bitcast.1, bf16[160,8,32,128]{3,2,1,0:T(8,128)(2,1)} %tiles_hbm.1), custom_call_target="tpu_custom_call" | custom-call | tf_op jit(solution)/shard_map/pallas_call | solution.py:290
  75.9 3.4 %copy.10 = f32[25,200,128]{2,1,0:T(8,128)} copy(f32[25,200,128]{2,1,0:T(8,128)} %shard_map.73) | data formatting | bytes 5120000

commit v2 on v0

v2 whole, which is shorter than its diff:
```python
import jax
import jax.numpy as jnp
from jax import lax
from jax.experimental import pallas as pl
from jax.experimental.pallas import tpu as pltpu
from jax.sharding import PartitionSpec as P

MESH = pl.DeviceIdType.MESH
SPREAD, MUT, NUT, KLW = 3, 8, 32, 128
NB, BATCH = 20, 8
TILES = NB * BATCH
NOCC, LOCAL, BLOCKS_MU = 200, 25, 192
NBF = BLOCKS_MU * MUT
PADDED = 208
STEP = 32
PIECES = 5
VMEM_LIMIT = 49 << 20
WIDTH = 5
COUNT = LOCAL // WIDTH
PAIRS = NB // 2 + 1
FRONT = 128
REAR = NOCC - FRONT
HALF = NBF // 2


def kernel(
    mu_hbm, nu_hbm, live_hbm, target_hbm, count_ref, own_hbm, tiles_hbm, out_ref,
    mu_ref, nu_ref, live_ref, target_ref, spots, own_ref,
    tiles, spread, gathered, staged, turned, across, quarter, running,
    held_front, held_rear, x_out, x_in, y_out, y_in, a_out, a_in, m_out, m_in, f_in,
    place, order, keep, small_sem, load_sem, own_sem, gather_send, gather_recv, send_sem, recv_sem,
):
    task, occ = lax.axis_index("task"), lax.axis_index("occ")
    z, y = task // 4, task % 4
    after = (task + 1) % 32
    before = (task + 31) % 32
    minus = (z + (y // 2) * (1 - y % 2)) % 8 * 4 + (y + 3) % 4
    minus_from = (z + 8 - (1 - y // 2) * (y % 2)) % 8 * 4 + (y + 1) % 4
    x, core = occ // 2, occ % 2
    right, left, far = (x + 1) % 4, (x + 3) % 4, (x + 2) % 4
    partner = x * 2 + 1 - core

    small = [
        pltpu.make_async_copy(source, target, small_sem.at[n])
        for n, (source, target) in enumerate(
            (
                (own_hbm, own_ref),
                (mu_hbm, mu_ref),
                (nu_hbm, nu_ref),
                (live_hbm, live_ref),
                (target_hbm, target_ref),
            )
        )
    ]
    for one in small:
        one.start()
    barrier = pltpu.get_barrier_semaphore()
    for other in (after, before, minus, minus_from):
        pl.semaphore_signal(barrier, inc=1, device_id={"task": other}, device_id_type=MESH)
    for other in (partner, right * 2 + core, left * 2 + core, far * 2 + core):
        pl.semaphore_signal(barrier, inc=1, device_id={"occ": other}, device_id_type=MESH)

    per_piece = TILES // PIECES

    def load(piece):
        return pltpu.make_async_copy(
            tiles_hbm.at[pl.ds(piece * per_piece, per_piece)],
            tiles.at[pl.ds(piece * per_piece, per_piece)],
            load_sem.at[piece],
        )

    small[0].wait()
    pl.semaphore_wait(barrier, 8)

    def give(source, target, index, other):
        return pltpu.make_async_remote_copy(
            src_ref=source, dst_ref=target,
            send_sem=gather_send.at[index], recv_sem=gather_recv.at[index],
            device_id={"occ": other}, device_id_type=MESH,
        )

    direct = [
        give(own_ref, gathered.at[core, x], n, other * 2 + core)
        for n, other in enumerate((right, left, far))
    ]
    over = [
        give(own_ref if n == 3 else gathered.at[core, slot], gathered.at[core, slot], 3 + n, partner)
        for n, slot in enumerate((left, right, far, x))
    ]
    for one in (direct[2], direct[0], direct[1], over[3]):
        one.start()
    keep_own = pltpu.make_async_copy(own_ref, gathered.at[core, x], own_sem)
    keep_own.start()
    for piece in range(PIECES):
        load(piece).start()

    row = lax.broadcasted_iota(jnp.int32, (128, 128), 0)
    lane = lax.broadcasted_iota(jnp.int32, (128, 128), 1)
    spreader = jnp.concatenate(
        [
            jnp.where(row == lane // 16 + 8 * v, 1.0, 0.0).astype(jnp.bfloat16)
            for v in range(16)
        ],
        axis=1,
    )

    def spread_block(block, carry):
        part = own_ref[:, pl.ds(pl.multiple_of(block * 128, 128), 128)]
        wide = jnp.dot(part, spreader, preferred_element_type=jnp.float32)
        for v in range(16):
            spread[block * 16 + v, :LOCAL] = wide[:, 128 * v : 128 * v + 128]
        return carry

    lax.fori_loop(0, 12, spread_block, 0)
    for n in range(2):
        direct[n].wait_recv()
        over[n].start()
    for one in small[1:]:
        one.wait()

    def spot(group, carry):
        for u in range(4):
            nu = nu_ref[group * 4 + u]
            turns = lax.rem(u + 4 - lax.rem(nu, 4), 4)
            spots[group * 4 + u] = turns * 12 + lax.div(nu, 4)
        return carry

    lax.fori_loop(0, TILES // 4, spot, 0)

    listed = count_ref[0]

    def count(b, found):
        t = target_ref[b]
        inside = jnp.where(b < listed, 1, 0)
        return tuple(n + jnp.where(t == s, inside, 0) for s, n in enumerate(found))

    zero = jnp.int32(0)
    found = lax.fori_loop(0, NB, count, (zero, zero, zero))
    pairs = [lax.div(n + 1, 2) for n in found]
    first_one, first_zero = pairs[2], pairs[2] + pairs[1]
    bases = (2 * first_zero, 2 * first_one, zero)

    def rank(b, seen):
        t = target_ref[b]
        inside = jnp.where(b < listed, 1, 0)
        at = jnp.where(t == 2, seen[2], jnp.where(t == 1, seen[1], seen[0]))
        place[b] = jnp.where(b < listed, at, -1)
        return tuple(n + jnp.where(t == s, inside, 0) for s, n in enumerate(seen))

    lax.fori_loop(0, NB, rank, bases)

    def fill(p, carry):
        held_by = jnp.int32(NB)
        for b in range(NB):
            held_by = jnp.where(place[b] == p, b, held_by)
        order[p] = held_by
        return carry

    lax.fori_loop(0, 2 * PAIRS, fill, 0)

    def runs(q, carry):
        fresh = jnp.where(q == first_one, 1, jnp.where(q == first_zero, 1, 0))
        keep[q] = (1 - fresh).astype(jnp.float32)
        return carry

    lax.fori_loop(0, PAIRS, runs, 0)
    ends = (first_zero + pairs[0], first_zero, first_one)
    final = [jnp.maximum(end - 1, 0) for end in ends]
    some = [jnp.where(n > 0, 1, 0).astype(jnp.float32) for n in pairs]


    row = lax.broadcasted_iota(jnp.int32, (16, 128), 0)
    lane = lax.broadcasted_iota(jnp.int32, (16, 128), 1)
    diagonal = jnp.where(lane % 16 == row, 1.0, 0.0).astype(jnp.bfloat16)

    def all_quarters(chunk):
        first = chunk * WIDTH
        slot = chunk % 2

        def inner(step, carry):
            for u in range(STEP):
                g = step * STEP + u
                mu = mu_ref[g]
                wide = jnp.concatenate(
                    [
                        jnp.broadcast_to(spread[mu, pl.ds(first + i, 1), :], (16, 128)).astype(
                            jnp.bfloat16
                        )
                        * diagonal
                        for i in range(WIDTH)
                    ],
                    axis=0,
                )
                block = tiles[g]
                both = jnp.concatenate(
                    [block[:, 16 * q : 16 * q + 16].reshape(128, 128) for q in range(2)], axis=1
                )
                product = jnp.dot(wide, both, preferred_element_type=jnp.float32)
                product = product.astype(jnp.bfloat16).reshape(WIDTH, 16, 256)
                for q in range(2):
                    start = u % BATCH * NUT + 16 * q
                    quarter[slot, :, step * (STEP // BATCH) + u // BATCH, start : start + 16, :] = product[
                        :, :, 128 * q : 128 * q + 128
                    ]
            return carry

        lax.fori_loop(0, TILES // STEP, inner, 0)

    for piece in range(PIECES):
        load(piece).wait()
    all_quarters(0)
    direct[2].wait_recv()
    over[2].start()
    all_quarters(1)
    keep_own.wait()
    for one in over:
        one.wait_recv()

    staged[NOCC:, :] = jnp.zeros((PADDED - NOCC, 128), jnp.float32)

    def turn(block, carry):
        where = pl.ds(pl.multiple_of(block * 128, 128), 128)
        for o in range(8):
            staged[25 * o : 25 * o + 25, :] = gathered[o % 2, o // 2, :, where].astype(jnp.float32)
        wide = staged[...]
        turned[block] = wide.astype(jnp.bfloat16)
        for r in range(1, 4):
            turned[r * 12 + block] = pltpu.roll(wide, 32 * r, 1).astype(jnp.bfloat16)
        return carry

    lax.fori_loop(0, 12, turn, 0)

    line = lax.broadcasted_iota(jnp.int32, (16, 128), 1) // 32
    quarter_lanes = [jnp.where(line == u, 1.0, 0.0) for u in range(4)]

    def gather(group, carry):
        merged = None
        for u in range(4):
            g = group * 4 + u
            mask = (quarter_lanes[u] * live_ref[g].astype(jnp.float32)).astype(jnp.bfloat16)
            mask = jnp.concatenate([mask] * (PADDED // 16), axis=0)
            part = turned[spots[g]] * mask
            merged = part if u == 0 else merged + part
        across[group // 2, group % 2] = merged
        return carry

    lax.fori_loop(0, TILES // 4, gather, 0)
    across[NB] = jnp.zeros((2, PADDED, 128), jnp.bfloat16)

    def all_sums(chunk):
        slot = chunk % 2
        for q in range(PAIRS):
            two = [order[2 * q + h] for h in range(2)]
            wide = jnp.concatenate([across[b, h] for b in two for h in range(2)], axis=1)
            rows = [jnp.minimum(b, NB - 1) for b in two]
            both = jnp.concatenate(
                [
                    jnp.concatenate([quarter[slot, i, at] for at in rows], axis=0)
                    for i in range(WIDTH)
                ],
                axis=1,
            )
            product = jnp.dot(wide, both, preferred_element_type=jnp.float32)
            for i in range(WIDTH):
                part = product[:NOCC, 128 * i : 128 * i + 128]
                if q > 0:
                    part = running[q - 1, i] * keep[q] + part
                running[q, i] = part

    def copy(source, target, kind, chunk, device):
        box = pl.ds(chunk * WIDTH, WIDTH)
        return pltpu.make_async_remote_copy(
            src_ref=source.at[box], dst_ref=target.at[box],
            send_sem=send_sem.at[kind, chunk], recv_sem=recv_sem.at[kind, chunk],
            device_id={"task": device}, device_id_type=MESH,
        )

    def copies(chunk):
        return (
            copy(x_out, x_in, 0, chunk, after),
            copy(y_out, y_in, 1, chunk, after),
            copy(a_out, a_in, 2, chunk, before),
            copy(m_out, m_in, 3, chunk, minus),
            copy(m_in, f_in, 4, chunk, minus),
        )

    def relay(chunk):
        send_x, send_y, send_a, send_m, _ = copies(chunk)
        send_a.wait_recv()
        for i in range(WIDTH):
            at = chunk * WIDTH + i
            m_out[at] = (held_rear[at] + a_in[at].astype(jnp.float32)).astype(jnp.bfloat16)
        send_m.start()
        send_x.wait_recv()
        for i in range(WIDTH):
            at = chunk * WIDTH + i
            y_out[at] = (held_front[at] + x_in[at].astype(jnp.float32)).astype(jnp.bfloat16)
        send_y.start()

    def forward(chunk):
        _, _, _, send_m, send_f = copies(chunk)
        send_m.wait_recv()
        send_f.start()

    def finish(chunk):
        _, send_y, _, _, send_f = copies(chunk)
        send_y.wait_recv()
        for i in range(WIDTH):
            at = chunk * WIDTH + i
            out_ref[at, :FRONT] = out_ref[at, :FRONT] + y_in[at].astype(jnp.float32)
        send_f.wait_recv()
        for i in range(WIDTH):
            at = chunk * WIDTH + i
            out_ref[at, FRONT:] = out_ref[at, FRONT:] + f_in[at].astype(jnp.float32)

    def body(chunk, carry):
        first = chunk * WIDTH

        all_sums(chunk)
        for i in range(WIDTH):
            two = running[final[2], i] * some[2]
            x_out[first + i] = two[:FRONT].astype(jnp.bfloat16)
            held_rear[first + i] = two[FRONT:]
        send_x, _, send_a, _, _ = copies(chunk)
        send_x.start()
        for i in range(WIDTH):
            one = running[final[1], i] * some[1]
            a_out[first + i] = one[FRONT:].astype(jnp.bfloat16)
            held_front[first + i] = one[:FRONT]
        send_a.start()
        for i in range(WIDTH):
            out_ref[first + i] = running[final[0], i] * some[0]

        @pl.when(chunk > 0)
        def _():
            relay(chunk - 1)

        @pl.when(chunk > 1)
        def _():
            forward(chunk - 2)

        @pl.when(jnp.logical_and(chunk > 0, chunk < COUNT - 1))
        def _():
            all_quarters(chunk + 1)

        return carry

    lax.fori_loop(0, COUNT, body, 0)
    relay(COUNT - 1)
    forward(COUNT - 2)

    def ending(chunk, carry):
        finish(chunk)
        return carry

    lax.fori_loop(0, COUNT - 2, ending, 0)
    forward(COUNT - 1)
    lax.fori_loop(COUNT - 2, COUNT, ending, 0)

    def drain(chunk, carry):
        for one in copies(chunk):
            one.wait_send()
        return carry

    lax.fori_loop(0, COUNT, drain, 0)
    for one in direct + over:
        one.wait_send()


def keep_out(array):
    return pltpu.with_memory_space_constraint(array, pltpu.HBM)


def local(ao_tiles, mo_coeffs, mu_blocks, nu_blocks, tile_live, batch_target, batch_count):
    hbm = pl.BlockSpec(memory_space=pltpu.HBM)
    front = pltpu.VMEM((LOCAL, FRONT, KLW), jnp.bfloat16)
    rear = pltpu.VMEM((LOCAL, REAR, KLW), jnp.bfloat16)
    return pl.pallas_call(
        kernel,
        out_shape=jax.ShapeDtypeStruct((LOCAL, NOCC, KLW), jnp.float32),
        in_specs=[hbm] * 4 + [pl.BlockSpec(memory_space=pltpu.SMEM)] + [hbm] * 2,
        out_specs=pl.BlockSpec(memory_space=pltpu.VMEM),
        scratch_shapes=[
            pltpu.SMEM((TILES,), jnp.int32),
            pltpu.SMEM((TILES,), jnp.int32),
            pltpu.SMEM((TILES,), jnp.int32),
            pltpu.SMEM((NB,), jnp.int32),
            pltpu.SMEM((TILES,), jnp.int32),
            pltpu.VMEM((LOCAL, NBF), jnp.bfloat16),
            pltpu.VMEM((TILES, MUT, NUT, KLW), jnp.bfloat16),
            pltpu.VMEM((BLOCKS_MU, 32, 128), jnp.float32),
            pltpu.VMEM((2, 4, LOCAL, NBF), jnp.bfloat16),
            pltpu.VMEM((PADDED, 128), jnp.float32),
            pltpu.VMEM((48, PADDED, 128), jnp.bfloat16),
            pltpu.VMEM((NB + 1, 2, PADDED, 128), jnp.bfloat16),
            pltpu.VMEM((2, WIDTH, NB, BATCH * NUT, KLW), jnp.bfloat16),
            pltpu.VMEM((PAIRS, WIDTH, NOCC, KLW), jnp.float32),
            pltpu.VMEM((LOCAL, FRONT, KLW), jnp.float32),
            pltpu.VMEM((LOCAL, REAR, KLW), jnp.float32),
            front, front, front, front,
            rear, rear, rear, rear, rear,
            pltpu.SMEM((NB,), jnp.int32),
            pltpu.SMEM((2 * PAIRS,), jnp.int32),
            pltpu.SMEM((PAIRS,), jnp.float32),
            pltpu.SemaphoreType.DMA((5,)),
            pltpu.SemaphoreType.DMA((PIECES,)),
            pltpu.SemaphoreType.DMA,
            pltpu.SemaphoreType.DMA((7,)),
            pltpu.SemaphoreType.DMA((7,)),
            pltpu.SemaphoreType.DMA((5, COUNT)),
            pltpu.SemaphoreType.DMA((5, COUNT)),
        ],
        compiler_params=pltpu.CompilerParams(
            vmem_limit_bytes=VMEM_LIMIT, collective_id=0, has_side_effects=True
        ),
    )(keep_out(mu_blocks), keep_out(nu_blocks), keep_out(tile_live), keep_out(batch_target), batch_count, keep_out(mo_coeffs.T), ao_tiles)


def solution(mesh):
    in_specs = (
        P("task", None, None, None),
        P(None, "occ"),
        P("task"),
        P("task"),
        P("task"),
        P("task"),
        P("task"),
    )
    out_specs = P("occ", None, "task")
    return jax.shard_map(local, mesh=mesh, in_specs=in_specs, out_specs=out_specs, check_vma=False)
```

time: 360 us -> 67.7 us (0.19)
  the two profiles are of different devices: /device:TPU:64 before, /device:TPU:1 now
where the time goes in v2:
time: 67.7 us; the launch traced here: 67.6 us
  Pallas kernels  65.5 us (97%)
  local copies, waits for them, and re-layouts  1.47 us (2%)
    pallas_call x1, Pallas kernels, local(): pl.pallas_call(kernel, out_shape=jax.ShapeDtypeStruct((LOCAL, NOCC, KLW),...  65.5 us
    unnamed x1, local copies, waits for them, and re-layouts  1.47 us

profile of v2, /device:TPU:1, one launch (start us, length us, event | category | flops | bytes accessed | tf_op | source)
XLA Modules:
  0.0 67.6 jit_solution(10848479189214826131)
XLA Ops:
  0.7 65.5 %shard_map.73 = f32[25,200,128]{2,1,0:T(8,128)S(1)} custom-call(s32[160]{0:T(256)} %mu_hbm.1, s32[160]{0:T(256)} %nu_hbm.1, s32[160]{0:T(256)} %live_hbm.1, s32[20]{0:T(128)} %target_hbm.1, s32[1]{0:T(128)S(6)} %copy.9.count_ref, bf16[25,1536]{1,0:T(8,128)(2,1)} %bitcast.1, bf16[160,8,32,128]{3,2,1,0:T(8,128)(2,1)} %tiles_hbm.1), custom_call_target="tpu_custom_call" | custom-call | tf_op jit(solution)/shard_map/pallas_call | solution.py:378
  66.1 1.5 %copy.10 = f32[25,200,128]{2,1,0:T(8,128)} copy(f32[25,200,128]{2,1,0:T(8,128)S(1)} %shard_map.73) | data formatting | bytes 5120000

commit v3 on v2

--- a/solution.py
+++ b/solution.py
@@ -223,9 +223,11 @@
         for o in range(8):
             staged[25 * o : 25 * o + 25, :] = gathered[o % 2, o // 2, :, where].astype(jnp.float32)
         wide = staged[...]
-        turned[block] = wide.astype(jnp.bfloat16)
+        turned[block] = wide.astype(jnp.bfloat16).reshape(PADDED // 16, 16, 128)
         for r in range(1, 4):
-            turned[r * 12 + block] = pltpu.roll(wide, 32 * r, 1).astype(jnp.bfloat16)
+            turned[r * 12 + block] = (
+                pltpu.roll(wide, 32 * r, 1).astype(jnp.bfloat16).reshape(PADDED // 16, 16, 128)
+            )
         return carry
 
     lax.fori_loop(0, 12, turn, 0)
@@ -233,25 +235,26 @@
     line = lax.broadcasted_iota(jnp.int32, (16, 128), 1) // 32
     quarter_lanes = [jnp.where(line == u, 1.0, 0.0) for u in range(4)]
 
-    def gather(group, carry):
-        merged = None
-        for u in range(4):
-            g = group * 4 + u
-            mask = (quarter_lanes[u] * live_ref[g].astype(jnp.float32)).astype(jnp.bfloat16)
-            mask = jnp.concatenate([mask] * (PADDED // 16), axis=0)
-            part = turned[spots[g]] * mask
-            merged = part if u == 0 else merged + part
-        across[group // 2, group % 2] = merged
-        return carry
-
-    lax.fori_loop(0, TILES // 4, gather, 0)
-    across[NB] = jnp.zeros((2, PADDED, 128), jnp.bfloat16)
+    def gather(batch, carry):
+        for half in range(2):
+            merged = None
+            for u in range(4):
+                g = batch * BATCH + half * 4 + u
+                mask = (quarter_lanes[u] * live_ref[g].astype(jnp.float32)).astype(jnp.bfloat16)
+                mask = jnp.concatenate([mask[None]] * (PADDED // 16), axis=0)
+                part = turned[spots[g]] * mask
+                merged = part if u == 0 else merged + part
+            across[batch, half] = merged
+        return carry
+
+    lax.fori_loop(0, NB, gather, 0)
+    across[NB] = jnp.zeros((2, PADDED // 16, 16, 128), jnp.bfloat16)
 
     def all_sums(chunk):
         slot = chunk % 2
         for q in range(PAIRS):
             two = [order[2 * q + h] for h in range(2)]
-            wide = jnp.concatenate([across[b, h] for b in two for h in range(2)], axis=1)
+            wide = jnp.concatenate([across[b, h].reshape(PADDED, 128) for b in two for h in range(2)], axis=1)
             rows = [jnp.minimum(b, NB - 1) for b in two]
             both = jnp.concatenate(
                 [
@@ -284,13 +287,16 @@
             copy(m_in, f_in, 4, chunk, minus),
         )
 
-    def relay(chunk):
-        send_x, send_y, send_a, send_m, _ = copies(chunk)
+    def relay_rear(chunk):
+        _, _, send_a, send_m, _ = copies(chunk)
         send_a.wait_recv()
         for i in range(WIDTH):
             at = chunk * WIDTH + i
             m_out[at] = (held_rear[at] + a_in[at].astype(jnp.float32)).astype(jnp.bfloat16)
         send_m.start()
+
+    def relay_front(chunk):
+        send_x, send_y, _, _, _ = copies(chunk)
         send_x.wait_recv()
         for i in range(WIDTH):
             at = chunk * WIDTH + i
@@ -333,20 +339,22 @@
 
         @pl.when(chunk > 0)
         def _():
-            relay(chunk - 1)
+            relay_front(chunk - 1)
+            relay_rear(chunk - 1)
+
+        @pl.when(jnp.logical_and(chunk > 0, chunk < COUNT - 1))
+        def _():
+            all_quarters(chunk + 1)
 
         @pl.when(chunk > 1)
         def _():
             forward(chunk - 2)
 
-        @pl.when(jnp.logical_and(chunk > 0, chunk < COUNT - 1))
-        def _():
-            all_quarters(chunk + 1)
-
         return carry
 
     lax.fori_loop(0, COUNT, body, 0)
-    relay(COUNT - 1)
+    relay_rear(COUNT - 1)
+    relay_front(COUNT - 1)
     forward(COUNT - 2)
 
     def ending(chunk, carry):
@@ -391,8 +399,8 @@
             pltpu.VMEM((BLOCKS_MU, 32, 128), jnp.float32),
             pltpu.VMEM((2, 4, LOCAL, NBF), jnp.bfloat16),
             pltpu.VMEM((PADDED, 128), jnp.float32),
-            pltpu.VMEM((48, PADDED, 128), jnp.bfloat16),
-            pltpu.VMEM((NB + 1, 2, PADDED, 128), jnp.bfloat16),
+            pltpu.VMEM((48, PADDED // 16, 16, 128), jnp.bfloat16),
+            pltpu.VMEM((NB + 1, 2, PADDED // 16, 16, 128), jnp.bfloat16),
             pltpu.VMEM((2, WIDTH, NB, BATCH * NUT, KLW), jnp.bfloat16),
             pltpu.VMEM((PAIRS, WIDTH, NOCC, KLW), jnp.float32),
             pltpu.VMEM((LOCAL, FRONT, KLW), jnp.float32),

time: 67.7 us -> 67.7 us (level)
  no operation moved by 1% of the time
where the time goes in v3:
time: 67.7 us; the launch traced here: 67.6 us
  Pallas kernels  65.4 us (97%)
  local copies, waits for them, and re-layouts  1.47 us (2%)
    pallas_call x1, Pallas kernels, local(): pl.pallas_call(kernel, out_shape=jax.ShapeDtypeStruct((LOCAL, NOCC, KLW),...  65.4 us
    unnamed x1, local copies, waits for them, and re-layouts  1.47 us

profile of v3, /device:TPU:1, one launch (start us, length us, event | category | flops | bytes accessed | tf_op | source)
XLA Modules:
  0.0 67.6 jit_solution(3179383670070514059)
XLA Ops:
  0.7 65.4 %shard_map.73 = f32[25,200,128]{2,1,0:T(8,128)S(1)} custom-call(s32[160]{0:T(256)} %mu_hbm.1, s32[160]{0:T(256)} %nu_hbm.1, s32[160]{0:T(256)} %live_hbm.1, s32[20]{0:T(128)} %target_hbm.1, s32[1]{0:T(128)S(6)} %copy.9.count_ref, bf16[25,1536]{1,0:T(8,128)(2,1)} %bitcast.1, bf16[160,8,32,128]{3,2,1,0:T(8,128)(2,1)} %tiles_hbm.1), custom_call_target="tpu_custom_call" | custom-call | tf_op jit(solution)/shard_map/pallas_call | solution.py:386
  66.1 1.5 %copy.10 = f32[25,200,128]{2,1,0:T(8,128)} copy(f32[25,200,128]{2,1,0:T(8,128)S(1)} %shard_map.73) | data formatting | bytes 5120000
